TPU v7x, 32 devices: a whole 2x2x4 slice. The times are simulated.
32 devices in a mesh: section: 4 (over x, core), tp: 8 (over z, y).
Axes of the slice: x: 2, y: 2, z: 4, core: 2. Of those that a mesh axis runs over, the one named last changes fastest.
Arguments:
- pending_activation: bfloat16 [4, 128, 4096], P('section'), may hold values from -6 to 6
- admissible_microbatches: bfloat16 [4, 128, 4096], P(None, None, 'tp'), may hold values from -6 to 6
- arrival_plan: int32 [4], replicated, may hold values from 0 to 3, each once
- vanished_hop: int32 [1], replicated, may hold values from 1 to 3
- query_key_value_matrices: bfloat16 [4, 4096, 3, 2048], P('section', None, None, 'tp')
- mixing_projection_matrices: bfloat16 [4, 2048, 4096], P('section', 'tp'), may hold values from -0.125 to 0.125
- normalizer_factors: bfloat16 [4, 4096], P('section'), may hold values from 0.25 to 1.75
Outputs:
- activation_later: bfloat16 [4, 128, 4096], P('section')
- standby_input: bfloat16 [4, 128, 4096], P('section', None, 'tp')
Inputs may be any that keep to these rules, and one draw needn't show every extreme that they name: `vanished_hop`: the preempted section is not the first. `arrival_plan`: each micro-batch index once.
All inputs are finite; a program needn't handle non-finite values.
Results may differ from a plain program's by a relative error of at most 0.013.
Values may be sent and summed in bfloat16 or wider, within the bound.
A program may use at most 64 MiB of HBM per device.

v0:
```python
import jax
import jax.numpy as jnp
from jax import lax
from jax.sharding import PartitionSpec as P

HD = 128
TICKS = 3
NORM_EPS = 1e-05


def shifted(value, axis, steps):
    count = lax.axis_size(axis)
    pairs = [(source, (source + steps) % count) for source in range(count)]
    return lax.ppermute(value, axis, pairs)


def layer_norm(x_rows, scale_row):
    widened = x_rows.astype(jnp.float32)
    row_mean = jnp.mean(widened, axis=-1, keepdims=True)
    centered = widened - row_mean
    row_var = jnp.mean(centered * centered, axis=-1, keepdims=True)
    return (centered * lax.rsqrt(row_var + NORM_EPS) * scale_row.astype(jnp.float32)).astype(
        jnp.bfloat16
    )


def attend(normed, w_in, w_out):
    row_count = normed.shape[0]
    col_count = w_in.shape[2]
    head_count = col_count // HD
    projected = jnp.dot(
        normed, w_in.reshape(w_in.shape[0], 3 * col_count), preferred_element_type=jnp.float32
    )
    projected = projected.astype(jnp.bfloat16).reshape(row_count, 3, head_count, HD)
    queries = projected[:, 0]
    key_rows = projected[:, 1]
    values = projected[:, 2]
    scores = jnp.einsum(
        "qhd,khd->hqk", queries, key_rows, preferred_element_type=jnp.float32
    ) * HD ** (-0.5)
    causal = jnp.arange(row_count)[:, None] >= jnp.arange(row_count)[None, :]
    scores = jnp.where(causal[None], scores, -jnp.inf)
    row_max = jnp.max(scores, axis=-1, keepdims=True)
    weights = jnp.exp(scores - row_max)
    probs = (weights / jnp.sum(weights, axis=-1, keepdims=True)).astype(jnp.bfloat16)
    context = jnp.einsum("hqk,khd->qhd", probs, values, preferred_element_type=jnp.float32)
    context = context.astype(jnp.bfloat16).reshape(row_count, col_count)
    return jnp.dot(context, w_out, preferred_element_type=jnp.float32)


def per_device(
    pending_activation,
    admissible_microbatches,
    arrival_plan,
    vanished_hop,
    query_key_value_matrices,
    mixing_projection_matrices,
    normalizer_factors,
):
    sections = lax.axis_size("section")
    my_section = lax.axis_index("section")
    sharding_degree = lax.axis_size("tp")
    slice_breadth = pending_activation.shape[2] // sharding_degree
    col_start = lax.axis_index("tp") * slice_breadth
    lost_at = vanished_hop[0]
    is_pred = my_section == lost_at - 1
    is_next = my_section == lost_at + 1
    is_lost = my_section == lost_at
    w_in = query_key_value_matrices[0]
    w_out = mixing_projection_matrices[0]
    scale_row = normalizer_factors[0]
    entire_source_lines = pending_activation[0]
    x_sh = lax.dynamic_slice_in_dim(entire_source_lines, col_start, slice_breadth, 1)
    blank = jnp.zeros(entire_source_lines.shape, jnp.float32)
    far_in, far_out, far_gain = shifted((w_in, w_out, scale_row), "section", -1)

    def successor_layer(rows_full):
        return attend(layer_norm(rows_full, far_gain), far_in, far_out)

    standby_sh = x_sh
    for tick_index in range(TICKS):
        own_part = attend(layer_norm(entire_source_lines, scale_row), w_in, w_out)
        ya_sh = (
            x_sh.astype(jnp.float32)
            + lax.psum_scatter(own_part, "tp", scatter_dimension=1, tiled=True)
        ).astype(jnp.bfloat16)
        ya_full = lax.all_gather(ya_sh, "tp", axis=1, tiled=True)
        spare_part = (
            successor_layer(ya_full)
            if tick_index == TICKS - 1
            else lax.cond(is_pred, lambda: successor_layer(ya_full), lambda: blank)
        )
        spare_sh = (
            ya_sh.astype(jnp.float32)
            + lax.psum_scatter(spare_part, "tp", scatter_dimension=1, tiled=True)
        ).astype(jnp.bfloat16)
        result_sh = jnp.where(is_pred, spare_sh, ya_sh)
        entering = lax.dynamic_index_in_dim(
            admissible_microbatches, arrival_plan[tick_index], 0, keepdims=False
        )
        send_sh = jnp.where(my_section == sections - 1, entering, result_sh)
        near_rows = shifted(send_sh, "section", 1)
        far_rows = shifted(spare_sh, "section", 2)
        x_sh = jnp.where(is_lost, jnp.zeros_like(far_rows), jnp.where(is_next, far_rows, near_rows))
        entire_source_lines = lax.all_gather(x_sh, "tp", axis=1, tiled=True)
        standby_sh = far_rows
    return (entire_source_lines[None], standby_sh[None])


def solution(mesh):
    placed = (
        P("section", None, None),
        P(None, None, "tp"),
        P(),
        P(),
        P("section", None, None, "tp"),
        P("section", "tp", None),
        P("section", None),
    )
    return jax.shard_map(
        per_device,
        mesh=mesh,
        in_specs=placed,
        out_specs=(P("section", None, None), P("section", None, "tp")),
        check_vma=False,
    )
```

profile of v0, /device:TPU:0, one launch (start us, length us, event | category | flops | bytes accessed | tf_op | source)
XLA Modules:
  0.0 769.3 jit_solution(308551706380850222)
XLA Ops:
  7.2 8.8 %copy.42 = bf16[1,4096,3,256]{1,3,2,0:T(8,128)(2,1)} copy(bf16[1,4096,3,256]{3,1,2,0:T(8,128)(2,1)} %param.15) | data formatting | bytes 12582912 | tf_op args[4]
  16.1 2.4 collective-permute-start.1
  19.9 5.2 convolution_convert_fusion.7
  26.5 1.8 fusion.103
  29.1 68.7 %reduce-scatter.7.cloned.1.call-done = f32[128,512]{1,0:T(8,128)} async-done(((f32[128,4096]{1,0:T(8,128)}), f32[128,512]{1,0:T(8,128)}) %reduce-scatter.7.cloned.1.call-update) | async-done | bytes 262160 | tf_op jit(solution)/shard_map/reduce_scatter | solution.py:85
  100.3 9.4 %collective-permute-done = bf16[4096]{0:T(1024)(128)(2,1)S(1)} collective-permute-done((bf16[4096]{0:T(1024)(128)(2,1)S(1)}, bf16[4096]{0:T(1024)(128)(2,1)S(1)}, u32[]{:S(2)}, u32[]{:S(2)}) %collective-permute-start) | collective-permute-done | bytes 8224 | tf_op jit(solution)/shard_map/ppermute | solution.py:14
  109.7 29.2 %all-gather.7.cloned.1.call-done = bf16[128,4096]{1,0:T(8,128)(2,1)} async-done(((bf16[128,512]{1,0:T(8,128)(2,1)}), bf16[128,4096]{1,0:T(8,128)(2,1)}) %all-gather.7.cloned.1.call-update) | async-done | bytes 1048592 | tf_op jit(solution)/shard_map/all_gather | solution.py:87
  138.9 12.4 %conditional.2 = (f32[128,4096]{1,0:T(8,128)}) conditional(s32[]{:T(128)} %convert_element_type.183, () %tuple.20, (bf16[128,4096]{1,0:T(8,128)(2,1)}, bf16[4096]{0:T(1024)(128)(2,1)S(1)}, bf16[4096,3,256]{0,2,1:T(8,128)(2,1)}, bf16[256,4096]{1,0:T(8,128)(2,1)}) %tuple.21), branch_computations={%region_5.6_spmd, %region_6.11_spmd} | conditional | flops 1096667776 | bytes 19741220 | solution.py:91
  142.2 5.0 convolution_convert_fusion
  148.0 3.4 fusion.118
  154.6 64.0 %reduce-scatter.9.cloned.1.call-done = f32[128,512]{1,0:T(8,128)} async-done(((f32[128,4096]{1,0:T(8,128)}), f32[128,512]{1,0:T(8,128)}) %reduce-scatter.9.cloned.1.call-update) | async-done | bytes 262160 | tf_op jit(solution)/shard_map/reduce_scatter | solution.py:95
  221.2 4.0 collective-permute-done.3
  226.8 38.5 %all-gather.9.cloned.1.call-done = bf16[128,4096]{1,0:T(8,128)(2,1)} async-done(((bf16[128,512]{1,0:T(8,128)(2,1)}), bf16[128,4096]{1,0:T(8,128)(2,1)}) %all-gather.9.cloned.1.call-update) | async-done | bytes 1048592 | tf_op jit(solution)/shard_map/all_gather | solution.py:105
  268.6 5.0 convolution_convert_fusion.6
  276.2 68.0 %reduce-scatter.11.cloned.1.call-done = f32[128,512]{1,0:T(8,128)} async-done(((f32[128,4096]{1,0:T(8,128)}), f32[128,512]{1,0:T(8,128)}) %reduce-scatter.11.cloned.1.call-update) | async-done | bytes 262160 | tf_op jit(solution)/shard_map/reduce_scatter | solution.py:85
  346.0 39.2 %all-gather.11.cloned.1.call-done = bf16[128,4096]{1,0:T(8,128)(2,1)} async-done(((bf16[128,512]{1,0:T(8,128)(2,1)}), bf16[128,4096]{1,0:T(8,128)(2,1)}) %all-gather.11.cloned.1.call-update) | async-done | bytes 1048592 | tf_op jit(solution)/shard_map/all_gather | solution.py:87
  385.2 12.4 %conditional.3 = (f32[128,4096]{1,0:T(8,128)}) conditional(s32[]{:T(128)} %convert_element_type.183, () %tuple.22, (bf16[128,4096]{1,0:T(8,128)(2,1)}, bf16[4096]{0:T(1024)(128)(2,1)S(1)}, bf16[4096,3,256]{0,2,1:T(8,128)(2,1)}, bf16[256,4096]{1,0:T(8,128)(2,1)}) %tuple.23), branch_computations={%region_17.18_spmd, %region_18.23_spmd} | conditional | flops 1096667776 | bytes 19741220 | solution.py:91
  388.4 5.0 convolution_convert_fusion.2
  394.2 3.4 fusion.119
  399.6 65.4 %reduce-scatter.13.cloned.1.call-done = f32[128,512]{1,0:T(8,128)} async-done(((f32[128,4096]{1,0:T(8,128)}), f32[128,512]{1,0:T(8,128)}) %reduce-scatter.13.cloned.1.call-update) | async-done | bytes 262160 | tf_op jit(solution)/shard_map/reduce_scatter | solution.py:95
  467.6 4.0 collective-permute-done.5
  473.3 38.5 %all-gather.13.cloned.1.call-done = bf16[128,4096]{1,0:T(8,128)(2,1)} async-done(((bf16[128,512]{1,0:T(8,128)(2,1)}), bf16[128,4096]{1,0:T(8,128)(2,1)}) %all-gather.13.cloned.1.call-update) | async-done | bytes 1048592 | tf_op jit(solution)/shard_map/all_gather | solution.py:105
  515.0 5.0 convolution_convert_fusion.5
  520.8 1.8 fusion.99
  522.7 68.3 %reduce-scatter.15.cloned.1.call-done = f32[128,512]{1,0:T(8,128)} async-done(((f32[128,4096]{1,0:T(8,128)}), f32[128,512]{1,0:T(8,128)}) %reduce-scatter.15.cloned.1.call-update) | async-done | bytes 262160 | tf_op jit(solution)/shard_map/reduce_scatter | solution.py:85
  592.7 39.2 %all-gather.15.cloned.1.call-done = bf16[128,4096]{1,0:T(8,128)(2,1)} async-done(((bf16[128,512]{1,0:T(8,128)(2,1)}), bf16[128,4096]{1,0:T(8,128)(2,1)}) %all-gather.15.cloned.1.call-update) | async-done | bytes 1048592 | tf_op jit(solution)/shard_map/all_gather | solution.py:87
  635.2 5.0 convolution_convert_fusion.4
  640.9 3.4 fusion.120
  646.5 66.3 %reduce-scatter.17.cloned.1.call-done = f32[128,512]{1,0:T(8,128)} async-done(((f32[128,4096]{1,0:T(8,128)}), f32[128,512]{1,0:T(8,128)}) %reduce-scatter.17.cloned.1.call-update) | async-done | bytes 262160 | tf_op jit(solution)/shard_map/reduce_scatter | solution.py:95
  715.3 4.1 collective-permute-done.7
  720.9 38.5 %all-gather.17.cloned.1.call-done = bf16[128,4096]{1,0:T(8,128)(2,1)} async-done(((bf16[128,512]{1,0:T(8,128)(2,1)}), bf16[128,4096]{1,0:T(8,128)(2,1)}) %all-gather.17.cloned.1.call-update) | async-done | bytes 1048592 | tf_op jit(solution)/shard_map/all_gather | solution.py:105
  759.5 2.3 copy.115
  (153 shorter events, 45.0 us)
Async XLA Ops:
  7.2 11.9 %copy-start.15 = (bf16[1,4096]{1,0:T(2,128)(2,1)S(1)}, bf16[1,4096]{1,0:T(2,128)(2,1)}, u32[]{:S(2)}) copy-start(bf16[1,4096]{1,0:T(2,128)(2,1)} %param.17) | copy-start | bytes 24580
  7.2 12.0 %copy-start.1 = (bf16[1,128,4096]{2,1,0:T(8,128)(2,1)S(1)}, bf16[1,128,4096]{2,1,0:T(8,128)(2,1)}, u32[]{:S(2)}) copy-start(bf16[1,128,4096]{2,1,0:T(8,128)(2,1)} %param.11) | copy-start | bytes 3145732
  7.2 90.7 %reduce-scatter.7.cloned.1.call-start = ((), (), s32[]{:S(2)}) async-start(), calls=%async_computation.6 | async-start | bytes 2359296 | tf_op jit(solution)/shard_map/reduce_scatter | solution.py:85
  16.1 122.9 %collective-permute-start.1 = (bf16[4096,3,256]{0,2,1:T(8,128)(2,1)}, bf16[4096,3,256]{0,2,1:T(8,128)(2,1)}, u32[]{:S(2)}, u32[]{:S(2)}) collective-permute-start(bf16[4096,3,256]{0,2,1:T(8,128)(2,1)} %bitcast.141), channel_id=1, source_target_pairs={{0,24},{8,0},{16,8},{24,16},{1,25},{9,1},{17,9},{25,17},{2,26},{10... | collective-permute-start | bytes 18874376 | tf_op jit(solution)/shard_map/ppermute | solution.py:14
  19.8 6.7 copy-start
  28.3 110.6 %all-gather.7.cloned.1.call-start = ((), (), s32[]{:S(2)}) async-start(), calls=%async_computation.7 | async-start | bytes 1179648 | tf_op jit(solution)/shard_map/all_gather | solution.py:87
  28.4 81.3 %collective-permute-start.2 = (bf16[256,4096]{1,0:T(8,128)(2,1)S(1)}, bf16[256,4096]{1,0:T(8,128)(2,1)}, u32[]{:S(2)}, u32[]{:S(2)}) collective-permute-start(bf16[256,4096]{1,0:T(8,128)(2,1)S(1)} %bitcast.140), channel_id=1, source_target_pairs={{0,24},{8,0},{16,8},{24,16},{1,25},{9,1},{17,9},{25,17},{2,26},{10... | collective-permute-start | bytes 6291464 | tf_op jit(solution)/shard_map/ppermute | solution.py:14
  99.5 119.0 %reduce-scatter.9.cloned.1.call-start = ((), (), s32[]{:S(2)}) async-start(), calls=%async_computation.8 | async-start | bytes 2359296 | tf_op jit(solution)/shard_map/reduce_scatter | solution.py:95
  99.6 10.2 %collective-permute-start = (bf16[4096]{0:T(1024)(128)(2,1)S(1)}, bf16[4096]{0:T(1024)(128)(2,1)S(1)}, u32[]{:S(2)}, u32[]{:S(2)}) collective-permute-start(bf16[4096]{0:T(1024)(128)(2,1)S(1)} %reduce.1), channel_id=1, source_target_pairs={{0,24},{8,0},{16,8},{24,16},{1,25},{9,1},{17,9},{25,17},{2,26},{10... | collective-permute-start | bytes 24584 | tf_op jit(solution)/shard_map/ppermute | solution.py:14
  151.4 67.2 %copy-start.7 = (bf16[128,512]{1,0:T(8,128)(2,1)S(1)}, bf16[128,512]{1,0:T(8,128)(2,1)}, u32[]{:S(2)}) copy-start(bf16[128,512]{1,0:T(8,128)(2,1)} %fusion.86) | copy-start | bytes 393220
  151.4 117.1 %copy-start.14 = (f32[4096]{0:T(1024)S(1)}, f32[4096]{0:T(1024)}, u32[]{:S(2)}) copy-start(f32[4096]{0:T(1024)} %copy-done.13) | copy-start | bytes 49156
  151.4 113.9 %all-gather.9.cloned.1.call-start = ((), (), s32[]{:S(2)}) async-start(), calls=%async_computation.9 | async-start | bytes 1179648 | tf_op jit(solution)/shard_map/all_gather | solution.py:105
  219.6 5.5 collective-permute-start.3
  221.2 4.9 collective-permute-start.4
  226.8 117.5 %reduce-scatter.11.cloned.1.call-start = ((), (), s32[]{:S(2)}) async-start(), calls=%async_computation.10 | async-start | bytes 2359296 | tf_op jit(solution)/shard_map/reduce_scatter | solution.py:85
  268.6 5.3 copy-start.16
  276.2 68.1 %copy-start.9 = (bf16[128,512]{1,0:T(8,128)(2,1)S(1)}, bf16[128,512]{1,0:T(8,128)(2,1)}, u32[]{:S(2)}) copy-start(bf16[128,512]{1,0:T(8,128)(2,1)} %select_select_fusion.2) | copy-start | bytes 393220
  276.2 109.0 %all-gather.11.cloned.1.call-start = ((), (), s32[]{:S(2)}) async-start(), calls=%async_computation.11 | async-start | bytes 1179648 | tf_op jit(solution)/shard_map/all_gather | solution.py:87
  345.9 119.2 %reduce-scatter.13.cloned.1.call-start = ((), (), s32[]{:S(2)}) async-start(), calls=%async_computation.12 | async-start | bytes 2359296 | tf_op jit(solution)/shard_map/reduce_scatter | solution.py:95
  397.6 67.5 %copy-start.10 = (bf16[128,512]{1,0:T(8,128)(2,1)S(1)}, bf16[128,512]{1,0:T(8,128)(2,1)}, u32[]{:S(2)}) copy-start(bf16[128,512]{1,0:T(8,128)(2,1)} %add_convert_fusion.3) | copy-start | bytes 393220
  397.6 67.5 %copy-start.12 = (bf16[4,128,512]{2,1,0:T(8,128)(2,1)S(1)}, bf16[4,128,512]{2,1,0:T(8,128)(2,1)}, u32[]{:S(2)}) copy-start(bf16[4,128,512]{2,1,0:T(8,128)(2,1)} %param.12) | copy-start | bytes 1572868
  397.6 114.2 %all-gather.13.cloned.1.call-start = ((), (), s32[]{:S(2)}) async-start(), calls=%async_computation.13 | async-start | bytes 1179648 | tf_op jit(solution)/shard_map/all_gather | solution.py:105
  466.1 5.5 collective-permute-start.5
  467.6 4.9 collective-permute-start.6
  473.2 117.7 %reduce-scatter.15.cloned.1.call-start = ((), (), s32[]{:S(2)}) async-start(), calls=%async_computation.14 | async-start | bytes 2359296 | tf_op jit(solution)/shard_map/reduce_scatter | solution.py:85
  522.6 68.4 %copy-start.8 = (bf16[128,512]{1,0:T(8,128)(2,1)S(1)}, bf16[128,512]{1,0:T(8,128)(2,1)}, u32[]{:S(2)}) copy-start(bf16[128,512]{1,0:T(8,128)(2,1)} %select_select_fusion.1) | copy-start | bytes 393220
  522.6 109.3 %all-gather.15.cloned.1.call-start = ((), (), s32[]{:S(2)}) async-start(), calls=%async_computation.15 | async-start | bytes 1179648 | tf_op jit(solution)/shard_map/all_gather | solution.py:87
  592.6 120.1 %reduce-scatter.17.cloned.1.call-start = ((), (), s32[]{:S(2)}) async-start(), calls=%async_computation.16 | async-start | bytes 2359296 | tf_op jit(solution)/shard_map/reduce_scatter | solution.py:95
  644.4 68.4 %copy-start.11 = (bf16[128,512]{1,0:T(8,128)(2,1)S(1)}, bf16[128,512]{1,0:T(8,128)(2,1)}, u32[]{:S(2)}) copy-start(bf16[128,512]{1,0:T(8,128)(2,1)} %add_convert_fusion.1) | copy-start | bytes 393220
  644.4 115.1 %all-gather.17.cloned.1.call-start = ((), (), s32[]{:S(2)}) async-start(), calls=%async_computation.17 | async-start | bytes 1179648 | tf_op jit(solution)/shard_map/all_gather | solution.py:105
  713.8 5.6 collective-permute-start.7
  715.3 4.9 collective-permute-start.8
  (7 other events, 17.4 us)
Sparse Core Ops, SparseCore 0:
  28.5 69.3 reduce-scatter.6
  100.5 38.4 all-gather.6
  151.5 66.9 reduce-scatter.8
  226.9 38.3 all-gather.8
  276.3 67.8 reduce-scatter.10
  346.7 38.3 all-gather.10
  397.7 67.2 reduce-scatter.12
  473.4 38.3 all-gather.12
  522.8 68.1 reduce-scatter.14
  593.4 38.4 all-gather.14
  644.5 68.2 reduce-scatter.16
  721.0 38.3 all-gather.16
where the time goes:
time: 771 us; the launch traced here: 769 us
  waiting for transfers between devices  648 us (84%)
  matrix products  48.7 us (6%)
  other arithmetic  27.9 us (4%)
  between operations  21.1 us (3%)
  local copies, waits for them, and re-layouts  14.9 us (2%)
  starting transfers between devices  8.26 us (1%)
    reduce_scatter x3, waiting for transfers between devices, per_device(): lax.psum_scatter(own_part, 'tp', scatter_dimension=1, tiled=True)  205 us
    reduce_scatter x3, waiting for transfers between devices, per_device(): lax.psum_scatter(spare_part, 'tp', scatter_dimension=1, tiled=True)  196 us
    all_gather x3, waiting for transfers between devices, per_device(): entire_source_lines = lax.all_gather(x_sh, 'tp', axis=1, tiled=True)  116 us
    all_gather x3, waiting for transfers between devices, per_device(): ya_full = lax.all_gather(ya_sh, 'tp', axis=1, tiled=True)  108 us
    dot_general x6, matrix products, attend(): jnp.dot(normed, w_in.reshape(w_in.shape[0], 3 * col_count), preferred_ele...  30.3 us
    ppermute x9, waiting for transfers between devices, shifted(): return lax.ppermute(value, axis, pairs)  24.2 us
    dot_general x6, matrix products, attend(): return jnp.dot(context, w_out, preferred_element_type=jnp.float32)  15.6 us
  transfers between devices with their start and end apart: 21, of which 19 were waited for; matrix products, arithmetic and copies ran while one was open for 2% of the time, Pallas kernels for 0%

commit v1 on v0

--- a/solution.py
+++ b/solution.py
@@ -6,6 +6,10 @@
 HD = 128
 TICKS = 3
 NORM_EPS = 1e-05
+build_the_entries = lambda x_part: jnp.concatenate(
+    lax.all_to_all(jnp.stack([x_part for _ in range(lax.axis_size("tp"))], axis=0), "tp", 0, 0),
+    axis=1,
+)
 
 
 def shifted(value, axis, steps):
@@ -84,7 +88,7 @@
             x_sh.astype(jnp.float32)
             + lax.psum_scatter(own_part, "tp", scatter_dimension=1, tiled=True)
         ).astype(jnp.bfloat16)
-        ya_full = lax.all_gather(ya_sh, "tp", axis=1, tiled=True)
+        ya_full = build_the_entries(ya_sh)
         spare_part = (
             successor_layer(ya_full)
             if tick_index == TICKS - 1

time: 771 us -> 738 us (0.957)
  waiting for transfers between devices: 648 us -> 603 us
  starting transfers between devices: 8.26 us -> 19.7 us
    all_gather x3 -> x0, waiting for transfers between devices: 108 us -> none  [per_device(): ya_full = lax.all_gather(ya_sh, 'tp', axis=1, tiled=True)]
    all_to_all x0 -> x3, waiting for transfers between devices: none -> 67.6 us  [lax.all_to_all(jnp.stack([x_part for _ in range(lax.axis_size('tp'))], ax...]
    all_to_all x0 -> x3, starting transfers between devices: none -> 11 us  [lax.all_to_all(jnp.stack([x_part for _ in range(lax.axis_size('tp'))], ax...]
where the time goes in v1:
time: 738 us; the launch traced here: 736 us
  waiting for transfers between devices  603 us (82%)
  matrix products  48.7 us (7%)
  other arithmetic  25.3 us (3%)
  between operations  20.5 us (3%)
  starting transfers between devices  19.7 us (3%)
  local copies, waits for them, and re-layouts  19.1 us (3%)
    reduce_scatter x3, waiting for transfers between devices, per_device(): lax.psum_scatter(own_part, 'tp', scatter_dimension=1, tiled=True)  205 us
    reduce_scatter x3, waiting for transfers between devices, per_device(): lax.psum_scatter(spare_part, 'tp', scatter_dimension=1, tiled=True)  195 us
    all_gather x3, waiting for transfers between devices, per_device(): entire_source_lines = lax.all_gather(x_sh, 'tp', axis=1, tiled=True)  115 us
    all_to_all x3, waiting for transfers between devices, lax.all_to_all(jnp.stack([x_part for _ in range(lax.axis_size('tp'))], ax...  67.6 us
    dot_general x6, matrix products, attend(): jnp.dot(normed, w_in.reshape(w_in.shape[0], 3 * col_count), preferred_ele...  30.2 us
    ppermute x9, waiting for transfers between devices, shifted(): return lax.ppermute(value, axis, pairs)  19.7 us
    dot_general x6, matrix products, attend(): return jnp.dot(context, w_out, preferred_element_type=jnp.float32)  15.6 us
  transfers between devices with their start and end apart: 21, of which 19 were waited for; matrix products, arithmetic and copies ran while one was open for 2% of the time, Pallas kernels for 0%

profile of v1, /device:TPU:0, one launch (start us, length us, event | category | flops | bytes accessed | tf_op | source)
XLA Modules:
  0.0 736.5 jit_solution(14723783247843376894)
XLA Ops:
  7.2 8.8 %copy.69 = bf16[1,4096,3,256]{1,3,2,0:T(8,128)(2,1)} copy(bf16[1,4096,3,256]{3,1,2,0:T(8,128)(2,1)} %param.15) | data formatting | bytes 12582912 | tf_op args[4]
  16.1 2.4 collective-permute-start.1
  19.8 5.2 convolution_convert_fusion.7
  29.1 69.1 %reduce-scatter.7.cloned.1.call-done = f32[128,512]{1,0:T(8,128)} async-done(((f32[128,4096]{1,0:T(8,128)}), f32[128,512]{1,0:T(8,128)}) %reduce-scatter.7.cloned.1.call-update) | async-done | bytes 262160 | tf_op jit(solution)/shard_map/reduce_scatter | solution.py:89
  100.2 3.7 all-to-all-start
  104.6 5.1 collective-permute-done
  109.7 18.6 %all-to-all-done = bf16[8,128,512]{2,1,0:T(8,128)(2,1)S(1)} async-done(((bf16[8,128,512]{2,1,0:T(8,128)(2,1)}), bf16[8,128,512]{2,1,0:T(8,128)(2,1)S(1)}, u32[]{:S(2)}, u32[]{:S(2)}) %all-to-all-start) | async-done | bytes 1048608 | tf_op jit(solution)/shard_map/all_to_all | solution.py:10
  128.3 13.2 %conditional.2 = (f32[128,4096]{1,0:T(8,128)}) conditional(s32[]{:T(128)} %convert_element_type.194, () %tuple.20, (bf16[128,8,512]{2,0,1:T(8,128)(2,1)S(1)}, bf16[4096]{0:T(1024)(128)(2,1)S(1)}, bf16[4096,3,256]{0,2,1:T(8,128)(2,1)}, bf16[256,4096]{1,0:T(8,128)(2,1)}) %tuple.68), branch_computations={%region_5.6_spmd, %region_6.11_spmd} | conditional | flops 1096663680 | bytes 19741192 | solution.py:95
  132.4 5.0 convolution_convert_fusion
  138.2 3.4 fusion.106
  144.8 63.7 %reduce-scatter.9.cloned.1.call-done = f32[128,512]{1,0:T(8,128)} async-done(((f32[128,4096]{1,0:T(8,128)}), f32[128,512]{1,0:T(8,128)}) %reduce-scatter.9.cloned.1.call-update) | async-done | bytes 262160 | tf_op jit(solution)/shard_map/reduce_scatter | solution.py:99
  211.1 4.0 collective-permute-done.3
  217.0 38.4 %all-gather.4.cloned.1.call-done = bf16[128,4096]{1,0:T(8,128)(2,1)} async-done(((bf16[128,512]{1,0:T(8,128)(2,1)}), bf16[128,4096]{1,0:T(8,128)(2,1)}) %all-gather.4.cloned.1.call-update) | async-done | bytes 1048592 | tf_op jit(solution)/shard_map/all_gather | solution.py:109
  258.6 5.0 convolution_convert_fusion.6
  266.2 68.0 %reduce-scatter.11.cloned.1.call-done = f32[128,512]{1,0:T(8,128)} async-done(((f32[128,4096]{1,0:T(8,128)}), f32[128,512]{1,0:T(8,128)}) %reduce-scatter.11.cloned.1.call-update) | async-done | bytes 262160 | tf_op jit(solution)/shard_map/reduce_scatter | solution.py:89
  336.2 3.7 all-to-all-start.1
  339.9 24.5 %all-to-all-done.1 = bf16[8,128,512]{2,1,0:T(8,128)(2,1)S(1)} async-done(((bf16[8,128,512]{2,1,0:T(8,128)(2,1)}), bf16[8,128,512]{2,1,0:T(8,128)(2,1)S(1)}, u32[]{:S(2)}, u32[]{:S(2)}) %all-to-all-start.1) | async-done | bytes 1048608 | tf_op jit(solution)/shard_map/all_to_all | solution.py:10
  364.5 13.2 %conditional.3 = (f32[128,4096]{1,0:T(8,128)}) conditional(s32[]{:T(128)} %convert_element_type.194, () %tuple.22, (bf16[128,8,512]{2,0,1:T(8,128)(2,1)S(1)}, bf16[4096]{0:T(1024)(128)(2,1)S(1)}, bf16[4096,3,256]{0,2,1:T(8,128)(2,1)}, bf16[256,4096]{1,0:T(8,128)(2,1)}) %tuple.69), branch_computations={%region_17.18_spmd, %region_18.23_spmd} | conditional | flops 1096663680 | bytes 19741192 | solution.py:95
  368.5 5.0 convolution_convert_fusion.2
  374.3 3.4 fusion.107
  379.5 65.2 %reduce-scatter.13.cloned.1.call-done = f32[128,512]{1,0:T(8,128)} async-done(((f32[128,4096]{1,0:T(8,128)}), f32[128,512]{1,0:T(8,128)}) %reduce-scatter.13.cloned.1.call-update) | async-done | bytes 262160 | tf_op jit(solution)/shard_map/reduce_scatter | solution.py:99
  447.2 4.0 collective-permute-done.5
  453.1 38.3 %all-gather.6.cloned.1.call-done = bf16[128,4096]{1,0:T(8,128)(2,1)} async-done(((bf16[128,512]{1,0:T(8,128)(2,1)}), bf16[128,4096]{1,0:T(8,128)(2,1)}) %all-gather.6.cloned.1.call-update) | async-done | bytes 1048592 | tf_op jit(solution)/shard_map/all_gather | solution.py:109
  494.6 5.0 convolution_convert_fusion.5
  502.3 68.4 %reduce-scatter.15.cloned.1.call-done = f32[128,512]{1,0:T(8,128)} async-done(((f32[128,4096]{1,0:T(8,128)}), f32[128,512]{1,0:T(8,128)}) %reduce-scatter.15.cloned.1.call-update) | async-done | bytes 262160 | tf_op jit(solution)/shard_map/reduce_scatter | solution.py:89
  572.9 3.6 all-to-all-start.2
  576.6 24.5 %all-to-all-done.2 = bf16[8,128,512]{1,2,0:T(8,128)(2,1)S(1)} async-done(((bf16[8,128,512]{1,2,0:T(8,128)(2,1)}), bf16[8,128,512]{1,2,0:T(8,128)(2,1)S(1)}, u32[]{:S(2)}, u32[]{:S(2)}) %all-to-all-start.2) | async-done | bytes 1048608 | tf_op jit(solution)/shard_map/all_to_all | solution.py:10
  602.9 5.0 convolution_convert_fusion.4
  608.7 3.4 fusion.108
  614.2 66.1 %reduce-scatter.17.cloned.1.call-done = f32[128,512]{1,0:T(8,128)} async-done(((f32[128,4096]{1,0:T(8,128)}), f32[128,512]{1,0:T(8,128)}) %reduce-scatter.17.cloned.1.call-update) | async-done | bytes 262160 | tf_op jit(solution)/shard_map/reduce_scatter | solution.py:99
  683.0 3.7 collective-permute-done.7
  688.4 38.6 %all-gather.8.cloned.1.call-done = bf16[128,4096]{1,0:T(8,128)(2,1)} async-done(((bf16[128,512]{1,0:T(8,128)(2,1)}), bf16[128,4096]{1,0:T(8,128)(2,1)}) %all-gather.8.cloned.1.call-update) | async-done | bytes 1048592 | tf_op jit(solution)/shard_map/all_gather | solution.py:109
  (147 shorter events, 53.1 us)
Async XLA Ops:
  7.2 11.9 %copy-start.9 = (bf16[1,4096]{1,0:T(2,128)(2,1)S(1)}, bf16[1,4096]{1,0:T(2,128)(2,1)}, u32[]{:S(2)}) copy-start(bf16[1,4096]{1,0:T(2,128)(2,1)} %param.17) | copy-start | bytes 24580
  7.2 12.0 %copy-start.1 = (bf16[1,128,4096]{2,1,0:T(8,128)(2,1)S(1)}, bf16[1,128,4096]{2,1,0:T(8,128)(2,1)}, u32[]{:S(2)}) copy-start(bf16[1,128,4096]{2,1,0:T(8,128)(2,1)} %param.11) | copy-start | bytes 3145732
  7.2 90.9 %reduce-scatter.7.cloned.1.call-start = ((), (), s32[]{:S(2)}) async-start(), calls=%async_computation.9 | async-start | bytes 2359296 | tf_op jit(solution)/shard_map/reduce_scatter | solution.py:89
  16.1 112.3 %collective-permute-start.1 = (bf16[4096,3,256]{0,2,1:T(8,128)(2,1)}, bf16[4096,3,256]{0,2,1:T(8,128)(2,1)}, u32[]{:S(2)}, u32[]{:S(2)}) collective-permute-start(bf16[4096,3,256]{0,2,1:T(8,128)(2,1)} %bitcast.155), channel_id=1, source_target_pairs={{0,24},{8,0},{16,8},{24,16},{1,25},{9,1},{17,9},{25,17},{2,26},{10... | collective-permute-start | bytes 18874376 | tf_op jit(solution)/shard_map/ppermute | solution.py:18
  19.1 0.7 copy-start.7
  19.8 6.7 copy-start
  28.3 81.4 %collective-permute-start.2 = (bf16[256,4096]{1,0:T(8,128)(2,1)S(1)}, bf16[256,4096]{1,0:T(8,128)(2,1)}, u32[]{:S(2)}, u32[]{:S(2)}) collective-permute-start(bf16[256,4096]{1,0:T(8,128)(2,1)S(1)} %bitcast.152), channel_id=1, source_target_pairs={{0,24},{8,0},{16,8},{24,16},{1,25},{9,1},{17,9},{25,17},{2,26},{10... | collective-permute-start | bytes 6291464 | tf_op jit(solution)/shard_map/ppermute | solution.py:18
  100.2 28.2 %all-to-all-start = ((bf16[8,128,512]{2,1,0:T(8,128)(2,1)}), bf16[8,128,512]{2,1,0:T(8,128)(2,1)S(1)}, u32[]{:S(2)}, u32[]{:S(2)}) async-start(bf16[8,128,512]{2,1,0:T(8,128)(2,1)} %stack.6), calls=%async_computation.1 | async-start | bytes 2097152 | tf_op jit(solution)/shard_map/all_to_all | solution.py:10
  103.8 104.7 %reduce-scatter.9.cloned.1.call-start = ((), (), s32[]{:S(2)}) async-start(), calls=%async_computation.10 | async-start | bytes 2359296 | tf_op jit(solution)/shard_map/reduce_scatter | solution.py:99
  103.9 5.9 collective-permute-start
  141.6 116.9 %copy-start.8 = (f32[4096]{0:T(1024)S(1)}, f32[4096]{0:T(1024)}, u32[]{:S(2)}) copy-start(f32[4096]{0:T(1024)} %copy-done.7) | copy-start | bytes 49156
  141.6 113.7 %all-gather.4.cloned.1.call-start = ((), (), s32[]{:S(2)}) async-start(), calls=%async_computation.11 | async-start | bytes 1179648 | tf_op jit(solution)/shard_map/all_gather | solution.py:109
  209.6 5.6 collective-permute-start.3
  211.1 4.9 collective-permute-start.4
  216.7 117.5 %reduce-scatter.11.cloned.1.call-start = ((), (), s32[]{:S(2)}) async-start(), calls=%async_computation.12 | async-start | bytes 2359296 | tf_op jit(solution)/shard_map/reduce_scatter | solution.py:89
  255.3 3.2 copy-start.3
  258.5 5.2 copy-start.10
  266.2 68.0 %copy-start.5 = (bf16[128,512]{1,0:T(8,128)(2,1)S(1)}, bf16[128,512]{1,0:T(8,128)(2,1)}, u32[]{:S(2)}) copy-start(bf16[128,512]{1,0:T(8,128)(2,1)} %select_select_fusion.2) | copy-start | bytes 393220
  336.2 28.2 %all-to-all-start.1 = ((bf16[8,128,512]{2,1,0:T(8,128)(2,1)}), bf16[8,128,512]{2,1,0:T(8,128)(2,1)S(1)}, u32[]{:S(2)}, u32[]{:S(2)}) async-start(bf16[8,128,512]{2,1,0:T(8,128)(2,1)} %stack.7), calls=%async_computation.4 | async-start | bytes 2097152 | tf_op jit(solution)/shard_map/all_to_all | solution.py:10
  339.9 104.8 %reduce-scatter.13.cloned.1.call-start = ((), (), s32[]{:S(2)}) async-start(), calls=%async_computation.13 | async-start | bytes 2359296 | tf_op jit(solution)/shard_map/reduce_scatter | solution.py:99
  377.7 67.0 %copy-start.6 = (bf16[4,128,512]{2,1,0:T(8,128)(2,1)S(1)}, bf16[4,128,512]{2,1,0:T(8,128)(2,1)}, u32[]{:S(2)}) copy-start(bf16[4,128,512]{2,1,0:T(8,128)(2,1)} %param.12) | copy-start | bytes 1572868
  377.7 113.7 %all-gather.6.cloned.1.call-start = ((), (), s32[]{:S(2)}) async-start(), calls=%async_computation.14 | async-start | bytes 1179648 | tf_op jit(solution)/shard_map/all_gather | solution.py:109
  445.7 5.5 collective-permute-start.5
  447.2 4.9 collective-permute-start.6
  452.8 117.8 %reduce-scatter.15.cloned.1.call-start = ((), (), s32[]{:S(2)}) async-start(), calls=%async_computation.15 | async-start | bytes 2359296 | tf_op jit(solution)/shard_map/reduce_scatter | solution.py:89
  491.4 3.2 copy-start.2
  502.3 68.4 %copy-start.4 = (bf16[128,512]{1,0:T(8,128)(2,1)S(1)}, bf16[128,512]{1,0:T(8,128)(2,1)}, u32[]{:S(2)}) copy-start(bf16[128,512]{1,0:T(8,128)(2,1)} %select_select_fusion.1) | copy-start | bytes 393220
  572.9 28.2 %all-to-all-start.2 = ((bf16[8,128,512]{1,2,0:T(8,128)(2,1)}), bf16[8,128,512]{1,2,0:T(8,128)(2,1)S(1)}, u32[]{:S(2)}, u32[]{:S(2)}) async-start(bf16[8,128,512]{1,2,0:T(8,128)(2,1)} %stack.8), calls=%async_computation.7 | async-start | bytes 2097152 | tf_op jit(solution)/shard_map/all_to_all | solution.py:10
  576.5 103.8 %reduce-scatter.17.cloned.1.call-start = ((), (), s32[]{:S(2)}) async-start(), calls=%async_computation.16 | async-start | bytes 2359296 | tf_op jit(solution)/shard_map/reduce_scatter | solution.py:99
  612.1 114.9 %all-gather.8.cloned.1.call-start = ((), (), s32[]{:S(2)}) async-start(), calls=%async_computation.17 | async-start | bytes 1179648 | tf_op jit(solution)/shard_map/all_gather | solution.py:109
  681.3 5.4 collective-permute-start.7
  683.0 4.7 collective-permute-start.8
  (1 other events, 0.7 us)
Sparse Core Ops, SparseCore 0:
  28.5 69.6 reduce-scatter.6
  141.7 66.7 reduce-scatter.8
  216.8 38.4 all-gather.3
  266.3 67.8 reduce-scatter.10
  377.9 66.7 reduce-scatter.12
  453.0 38.4 all-gather.5
  502.4 68.1 reduce-scatter.14
  612.2 68.0 reduce-scatter.16
  688.6 38.4 all-gather.7
